TPU v7x, 32 devices: a whole 2x2x4 slice. The times are simulated.
32 devices in a mesh: groups: 2 (over y), section: 4 (over z), seq: 4 (over x, core).
Axes of the slice: x: 2, y: 2, z: 4, core: 2. Of those that a mesh axis runs over, the one named last changes fastest.
Arguments:
- tokens: bfloat16 [8, 256, 1440], P('groups', 'seq'), parts along dimension 0, may hold values from -6 to 6
- block_order: int32 [8], P('groups'), parts along dimension 0, may hold values from 0 to 3, each once
- prompt_lengths: int32 [8], P('groups'), parts along dimension 0, may hold values from 1 to 256, 576 in all
- norm_gain: float32 [4, 1440], P('section'), may hold values from 0.1 to 1.9
- w_query: bfloat16 [4, 1440, 2048], P('section', None, 'seq'), may hold values from -4 to 4
- w_key_value: bfloat16 [4, 1440, 512], P('section'), may hold values from -4 to 4
- w_out: bfloat16 [4, 2048, 1440], P('section', 'seq'), may hold values from -0.125 to 0.125
- sink_logits: float32 [4, 32], P('section'), may hold values from 0 to 4
Outputs:
- hidden_states: bfloat16 [4, 8, 256, 1440], P('section', 'groups', 'seq'), parts along dimension 1
- layer_cache: bfloat16 [4, 8, 256, 512], P('section', 'groups', 'seq'), parts along dimension 1
There are 2 independent parts, one for each index of `groups`. A program takes and returns all parts, laid end to end along the dimension named above; an argument that names none is the same for every part. Nothing has to cross between parts.
Inputs may be any that keep to these rules, and one draw needn't show every extreme that they name: `block_order`: each of 0 to 3 exactly once. `prompt_lengths`: the longest prompt is full.
All inputs are finite; a program needn't handle non-finite values.
Results may differ from a plain program's by a relative error of at most 0.024.
Values may be sent and summed in bfloat16 or wider, within the bound.
No kernel may reach another device: no remote copies, remote signals or barrier semaphores. Data moves between devices by JAX's collectives and lax.ppermute only.
A program may use at most 128 MiB of HBM per device.

v0:
```python
import math
import jax
import jax.numpy as jnp
from jax import lax
from jax.sharding import PartitionSpec as P

HEAD_DIM = 64
WIN = 128
THETA = 150000.0
EPSILON = 1e-05


def from_behind(block, axis, distance):
    devices = range(lax.axis_size(axis))
    route = [(i - distance, i) for i in devices if i - distance in devices]
    return lax.ppermute(block, axis, route)


def rotary(positions, head_size):
    half = head_size // 2
    freq = jnp.exp(jnp.arange(half, dtype=jnp.float32) * (-2.0 * math.log(THETA) / head_size))
    angles = positions.astype(jnp.float32)[:, None] * freq[None, :]
    return (jnp.cos(angles)[:, None, :], jnp.sin(angles)[:, None, :])


def rotate(values, cosine, sine):
    half = values.shape[-1] // 2
    first = values[..., :half]
    second = values[..., half:]
    return jnp.concatenate([first * cosine - second * sine, second * cosine + first * sine], -1)


def per_device(
    tokens, block_order, prompt_lengths, norm_gain, w_query, w_key_value, w_out, sink_logits
):
    section_index = lax.axis_index("section")
    sections = lax.axis_size("section")
    seq_index = lax.axis_index("seq")
    micro, rows, width = tokens.shape
    full_query, full_out = (
        lax.all_gather(w_query, "seq", axis=2, tiled=True),
        lax.all_gather(w_out, "seq", axis=1, tiled=True),
    )
    query_weight = full_query[0]
    out_weight = full_out[0]
    pair_weight = w_key_value[0]
    gain = norm_gain[0]
    heads_width = query_weight.shape[1]
    head_count = heads_width // HEAD_DIM
    kv_width = pair_weight.shape[1] // 2
    kv_heads = kv_width // HEAD_DIM
    group = head_count // kv_heads
    sink = sink_logits[0].reshape(kv_heads, group)[:, :, None]
    keep = min(WIN, rows)
    depth = WIN // keep
    start = seq_index * rows
    positions = start + jnp.arange(rows, dtype=jnp.int32)
    cosine, sine = rotary(positions, HEAD_DIM)
    key_positions = start - WIN + jnp.arange(WIN + rows, dtype=jnp.int32)

    def project(hidden):
        widened = hidden.astype(jnp.float32)
        scale = lax.rsqrt(jnp.mean(widened * widened, -1, keepdims=True) + EPSILON)
        normed = (widened * scale * gain).astype(jnp.bfloat16)
        queries = jnp.dot(normed, query_weight, preferred_element_type=jnp.float32).reshape(
            rows, head_count, HEAD_DIM
        )
        queries = rotate(queries, cosine, sine).astype(jnp.bfloat16).reshape(rows, heads_width)
        projected = jnp.dot(normed, pair_weight, preferred_element_type=jnp.float32)
        rotated = rotate(
            projected[:, :kv_width].reshape(rows, kv_heads, HEAD_DIM), cosine, sine
        ).reshape(rows, kv_width)
        cache = jnp.concatenate([rotated, projected[:, kv_width:]], 1).astype(jnp.bfloat16)
        return (queries, cache)

    def project_spare(hidden):
        return (
            jnp.zeros((rows, heads_width), jnp.bfloat16),
            jnp.zeros((rows, 2 * kv_width), jnp.bfloat16),
        )

    def window_of(cache):
        pieces = [from_behind(cache, "seq", offset) for offset in range(depth, 0, -1)]
        return jnp.concatenate(pieces, 0)

    def attend(operands):
        hidden, queries, cache, window, length = operands
        joined = jnp.concatenate([window, cache], 0)
        key_heads = joined[:, :kv_width].reshape(WIN + rows, kv_heads, HEAD_DIM)
        value_heads = joined[:, kv_width:].reshape(WIN + rows, kv_heads, HEAD_DIM)
        grouped = queries.reshape(rows, kv_heads, group, HEAD_DIM)
        scores = (
            jnp.einsum("qkgd,skd->kgqs", grouped, key_heads, preferred_element_type=jnp.float32)
            * 0.125
        )
        query_col = positions[:, None]
        key_row = key_positions[None, :]
        allowed = (key_row <= query_col) & (query_col - key_row < WIN) & (key_row >= 0)
        allowed = allowed & ((key_row < length) | (key_row == query_col))
        masked = jnp.where(allowed, scores, jnp.float32(-1e30))
        top = jnp.maximum(jnp.max(masked, -1), sink)
        expo = jnp.where(allowed, jnp.exp(scores - top[..., None]), jnp.float32(0.0))
        total = jnp.sum(expo, -1) + jnp.exp(sink - top)
        weights = (expo / total[..., None]).astype(jnp.bfloat16)
        context = jnp.einsum(
            "kgqs,skd->qkgd", weights, value_heads, preferred_element_type=jnp.float32
        )
        context = context.reshape(rows, heads_width).astype(jnp.bfloat16)
        output = jnp.dot(context, out_weight, preferred_element_type=jnp.float32)
        return (hidden.astype(jnp.float32) + output).astype(jnp.bfloat16)

    def pass_through(operands):
        return operands[0]

    def turn(counter, carry):
        arriving, hidden_buffer, cache_buffer = carry
        slot = counter - section_index
        active = (slot >= 0) & (slot < micro)
        slot_safe = jnp.clip(slot, 0, micro - 1)
        block = block_order[slot_safe]
        length = prompt_lengths[block]
        entering = lax.dynamic_index_in_dim(tokens, block, 0, keepdims=False)
        hidden = jnp.where(section_index == 0, entering, arriving)
        queries, cache = lax.cond(active, project, project_spare, hidden)
        window = window_of(cache)
        updated = lax.cond(active, attend, pass_through, (hidden, queries, cache, window, length))
        previous_hidden = lax.dynamic_index_in_dim(hidden_buffer, slot_safe, 0, keepdims=False)
        previous_cache = lax.dynamic_index_in_dim(cache_buffer, slot_safe, 0, keepdims=False)
        hidden_buffer = lax.dynamic_update_index_in_dim(
            hidden_buffer, jnp.where(active, updated, previous_hidden), slot_safe, 0
        )
        cache_buffer = lax.dynamic_update_index_in_dim(
            cache_buffer, jnp.where(active, cache, previous_cache), slot_safe, 0
        )
        passed = from_behind(updated, "section", 1)
        return (passed, hidden_buffer, cache_buffer)

    initial = (
        jnp.zeros((rows, width), jnp.bfloat16),
        jnp.zeros((micro, rows, width), jnp.bfloat16),
        jnp.zeros((micro, rows, 2 * kv_width), jnp.bfloat16),
    )
    final = lax.fori_loop(0, micro + sections - 1, turn, initial)
    return (final[1][None], final[2][None])


def solution(mesh):
    in_specs = (
        P("groups", "seq", None),
        P("groups"),
        P("groups"),
        P("section", None),
        P("section", None, "seq"),
        P("section", None, None),
        P("section", "seq", None),
        P("section", None),
    )
    out_specs = (P("section", "groups", "seq", None), P("section", "groups", "seq", None))
    return jax.shard_map(
        per_device, mesh=mesh, in_specs=in_specs, out_specs=out_specs, check_vma=False
    )
```

profile of v0, /device:TPU:28, one launch (start us, length us, event | category | flops | bytes accessed | tf_op | source)
XLA Modules:
  0.0 363.9 jit_solution(2830805438816558788)
XLA Ops:
  8.5 1.6 copy.14
  11.5 43.2 %all-gather.3.cloned.1.call-done = bf16[1,1440,2048]{2,1,0:T(8,128)(2,1)} async-done(((bf16[1,1440,512]{2,1,0:T(8,128)(2,1)}), bf16[1,1440,2048]{2,1,0:T(8,128)(2,1)}) %all-gather.3.cloned.1.call-update) | async-done | bytes 5898256 | tf_op jit(solution)/shard_map/all_gather | solution.py:41
  54.6 47.9 %all-gather.5.cloned.1.call-done = bf16[1,2048,1440]{2,1,0:T(8,128)(2,1)} async-done(((bf16[1,512,1440]{2,1,0:T(8,128)(2,1)}), bf16[1,2048,1440]{2,1,0:T(8,128)(2,1)}) %all-gather.5.cloned.1.call-update) | async-done | bytes 5898256 | tf_op jit(solution)/shard_map/all_gather | solution.py:42
  104.3 252.8 %while.20 = (s32[]{:T(128)}, bf16[64,1440]{1,0:T(8,128)(2,1)S(1)}, bf16[4,64,1440]{2,1,0:T(8,128)(2,1)}, bf16[4,64,512]{2,1,0:T(8,128)(2,1)}, s32[]{:T(128)}, /*...) while((s32[]{:T(128)}, bf16[64,1440]{1,0:T(8,128)(2,1)S(1)}, ...), condition=%wide.region_8.9_spmd.clone.clone, body=%wide.region_0.8_spmd.clone.clone.sunk | while | flops 958372544 | bytes 47880768 | solution.py:143
  107.8 1.4 conditional.8
  109.1 2.5 collective-permute-start
  111.6 1.9 collective-permute-start.1
  116.0 1.3 collective-permute-start.2
  118.0 7.3 %collective-permute-done.2 = bf16[64,1440]{1,0:T(8,128)(2,1)S(1)} collective-permute-done((bf16[64,1440]{1,0:T(8,128)(2,1)S(1)}, bf16[64,1440]{1,0:T(8,128)(2,1)S(1)}, u32[]{:S(2)}, u32[]{:S(2)}) %collective-permute-start.2) | collective-permute-done | bytes 184352 | tf_op jit(solution)/shard_map/while/body/eval_jaxpr/ppermute | solution.py:16
  128.8 1.4 conditional.8
  130.1 3.0 collective-permute-start
  133.2 1.3 collective-permute-start.1
  137.0 1.3 collective-permute-start.2
  139.0 7.2 %collective-permute-done.2 = bf16[64,1440]{1,0:T(8,128)(2,1)S(1)} collective-permute-done((bf16[64,1440]{1,0:T(8,128)(2,1)S(1)}, bf16[64,1440]{1,0:T(8,128)(2,1)S(1)}, u32[]{:S(2)}, u32[]{:S(2)}) %collective-permute-start.2) | collective-permute-done | bytes 184352 | tf_op jit(solution)/shard_map/while/body/eval_jaxpr/ppermute | solution.py:16
  149.6 1.4 conditional.8
  151.0 3.0 collective-permute-start
  154.0 1.3 collective-permute-start.1
  157.8 1.3 collective-permute-start.2
  159.8 50.5 %collective-permute-done.2 = bf16[64,1440]{1,0:T(8,128)(2,1)S(1)} collective-permute-done((bf16[64,1440]{1,0:T(8,128)(2,1)S(1)}, bf16[64,1440]{1,0:T(8,128)(2,1)S(1)}, u32[]{:S(2)}, u32[]{:S(2)}) %collective-permute-start.2) | collective-permute-done | bytes 184352 | tf_op jit(solution)/shard_map/while/body/eval_jaxpr/ppermute | solution.py:16
  213.8 9.2 %conditional.8 = (bf16[64,2048]{1,0:T(8,128)(2,1)S(1)}, bf16[64,512]{1,0:T(8,128)(2,1)}, bf16[64,512]{0,1:T(8,128)(2,1)}) conditional(s32[]{:T(128)} %convert_element_type.69, () %tuple.79, (bf16[64,1440]{1,0:T(8,128)(2,1)S(1)}, f32[1,1440]{1,0:T(1,128)S(1)}, bf16[1440,2048]{1,0:T(8,128)(2,1)}, f32[64,1,32]{2,0,1:T(8,128)S(1)}, ...), branch_computations={%region_1.1_spmd, %region_2.3_spmd} | conditional | flops 474183744 | bytes 12373788 | solution.py:124
  214.0 3.9 %fusion.26 = f32[64,2048]{1,0:T(8,128)S(1)} fusion(bf16[1440,2048]{1,0:T(8,128)(2,1)} %get-tuple-element.374, bf16[64,1440]{1,0:T(8,128)(2,1)S(1)} %get-tuple-element.372, f32[1440]{0:T(1024)S(1)} %reduce, f32[64]{0:T(128)S(1)} %add_rsqrt_fusion), kind=kOutput, calls=%fused_computation.44 | convolution fusion | flops 377856000 | bytes 6612864 | tf_op jit(solution)/shard_map/while/body/eval_jaxpr/cond/branch_1_fun/dot_general | solution.py:65
  221.4 1.6 copy.18
  223.0 2.3 collective-permute-start
  225.4 1.3 collective-permute-start.1
  228.5 1.5 bitcast_dynamic-update-slice_fusion.5
  230.0 8.0 %conditional.9 = (bf16[64,1440]{1,0:T(8,128)(2,1)S(1)}) conditional(s32[]{:T(128)} %convert_element_type.69, bf16[64,1440]{1,0:T(8,128)(2,1)S(1)} %bitcast_select_fusion.5, (bf16[64,1440]{1,0:T(8,128)(2,1)S(1)}, bf16[64,512]{0,1:T(8,128)(2,1)S(1)}, bf16[64,512]{0,1:T(8,128)(2,1)S(1)}, bf16[64,512]{1,0:T(8,128)(2,1)}, s32[]{:T(128)}, ...), branch_computations={%region_4.4_spmd, %region_5.7_spmd} | conditional | flops 483969664 | bytes 32420688 | solution.py:126
  234.5 1.1 convolution_convert_fusion
  236.7 1.2 fusion.8
  238.0 1.3 collective-permute-start.2
  240.0 7.1 %collective-permute-done.2 = bf16[64,1440]{1,0:T(8,128)(2,1)S(1)} collective-permute-done((bf16[64,1440]{1,0:T(8,128)(2,1)S(1)}, bf16[64,1440]{1,0:T(8,128)(2,1)S(1)}, u32[]{:S(2)}, u32[]{:S(2)}) %collective-permute-start.2) | collective-permute-done | bytes 184352 | tf_op jit(solution)/shard_map/while/body/eval_jaxpr/ppermute | solution.py:16
  250.6 9.2 %conditional.8 = (bf16[64,2048]{1,0:T(8,128)(2,1)S(1)}, bf16[64,512]{1,0:T(8,128)(2,1)}, bf16[64,512]{0,1:T(8,128)(2,1)}) conditional(s32[]{:T(128)} %convert_element_type.69, () %tuple.79, (bf16[64,1440]{1,0:T(8,128)(2,1)S(1)}, f32[1,1440]{1,0:T(1,128)S(1)}, bf16[1440,2048]{1,0:T(8,128)(2,1)}, f32[64,1,32]{2,0,1:T(8,128)S(1)}, ...), branch_computations={%region_1.1_spmd, %region_2.3_spmd} | conditional | flops 474183744 | bytes 12373788 | solution.py:124
  250.8 3.9 %fusion.26 = f32[64,2048]{1,0:T(8,128)S(1)} fusion(bf16[1440,2048]{1,0:T(8,128)(2,1)} %get-tuple-element.374, bf16[64,1440]{1,0:T(8,128)(2,1)S(1)} %get-tuple-element.372, f32[1440]{0:T(1024)S(1)} %reduce, f32[64]{0:T(128)S(1)} %add_rsqrt_fusion), kind=kOutput, calls=%fused_computation.44 | convolution fusion | flops 377856000 | bytes 6612864 | tf_op jit(solution)/shard_map/while/body/eval_jaxpr/cond/branch_1_fun/dot_general | solution.py:65
  258.2 1.6 copy.18
  259.8 2.3 collective-permute-start
  262.1 1.3 collective-permute-start.1
  265.2 1.5 bitcast_dynamic-update-slice_fusion.5
  266.7 8.0 %conditional.9 = (bf16[64,1440]{1,0:T(8,128)(2,1)S(1)}) conditional(s32[]{:T(128)} %convert_element_type.69, bf16[64,1440]{1,0:T(8,128)(2,1)S(1)} %bitcast_select_fusion.5, (bf16[64,1440]{1,0:T(8,128)(2,1)S(1)}, bf16[64,512]{0,1:T(8,128)(2,1)S(1)}, bf16[64,512]{0,1:T(8,128)(2,1)S(1)}, bf16[64,512]{1,0:T(8,128)(2,1)}, s32[]{:T(128)}, ...), branch_computations={%region_4.4_spmd, %region_5.7_spmd} | conditional | flops 483969664 | bytes 32420688 | solution.py:126
  266.7 1.0 copy.13
  271.3 1.1 convolution_convert_fusion
  273.5 1.2 fusion.8
  274.7 1.3 collective-permute-start.2
  276.8 7.1 %collective-permute-done.2 = bf16[64,1440]{1,0:T(8,128)(2,1)S(1)} collective-permute-done((bf16[64,1440]{1,0:T(8,128)(2,1)S(1)}, bf16[64,1440]{1,0:T(8,128)(2,1)S(1)}, u32[]{:S(2)}, u32[]{:S(2)}) %collective-permute-start.2) | collective-permute-done | bytes 184352 | tf_op jit(solution)/shard_map/while/body/eval_jaxpr/ppermute | solution.py:16
  287.3 9.2 %conditional.8 = (bf16[64,2048]{1,0:T(8,128)(2,1)S(1)}, bf16[64,512]{1,0:T(8,128)(2,1)}, bf16[64,512]{0,1:T(8,128)(2,1)}) conditional(s32[]{:T(128)} %convert_element_type.69, () %tuple.79, (bf16[64,1440]{1,0:T(8,128)(2,1)S(1)}, f32[1,1440]{1,0:T(1,128)S(1)}, bf16[1440,2048]{1,0:T(8,128)(2,1)}, f32[64,1,32]{2,0,1:T(8,128)S(1)}, ...), branch_computations={%region_1.1_spmd, %region_2.3_spmd} | conditional | flops 474183744 | bytes 12373788 | solution.py:124
  287.5 3.9 %fusion.26 = f32[64,2048]{1,0:T(8,128)S(1)} fusion(bf16[1440,2048]{1,0:T(8,128)(2,1)} %get-tuple-element.374, bf16[64,1440]{1,0:T(8,128)(2,1)S(1)} %get-tuple-element.372, f32[1440]{0:T(1024)S(1)} %reduce, f32[64]{0:T(128)S(1)} %add_rsqrt_fusion), kind=kOutput, calls=%fused_computation.44 | convolution fusion | flops 377856000 | bytes 6612864 | tf_op jit(solution)/shard_map/while/body/eval_jaxpr/cond/branch_1_fun/dot_general | solution.py:65
  294.9 1.6 copy.18
  296.5 2.3 collective-permute-start
  298.9 1.3 collective-permute-start.1
  302.0 1.5 bitcast_dynamic-update-slice_fusion.5
  303.5 8.0 %conditional.9 = (bf16[64,1440]{1,0:T(8,128)(2,1)S(1)}) conditional(s32[]{:T(128)} %convert_element_type.69, bf16[64,1440]{1,0:T(8,128)(2,1)S(1)} %bitcast_select_fusion.5, (bf16[64,1440]{1,0:T(8,128)(2,1)S(1)}, bf16[64,512]{0,1:T(8,128)(2,1)S(1)}, bf16[64,512]{0,1:T(8,128)(2,1)S(1)}, bf16[64,512]{1,0:T(8,128)(2,1)}, s32[]{:T(128)}, ...), branch_computations={%region_4.4_spmd, %region_5.7_spmd} | conditional | flops 483969664 | bytes 32420688 | solution.py:126
  308.0 1.1 convolution_convert_fusion
  310.2 1.2 fusion.8
  311.5 1.3 collective-permute-start.2
  313.5 7.1 %collective-permute-done.2 = bf16[64,1440]{1,0:T(8,128)(2,1)S(1)} collective-permute-done((bf16[64,1440]{1,0:T(8,128)(2,1)S(1)}, bf16[64,1440]{1,0:T(8,128)(2,1)S(1)}, u32[]{:S(2)}, u32[]{:S(2)}) %collective-permute-start.2) | collective-permute-done | bytes 184352 | tf_op jit(solution)/shard_map/while/body/eval_jaxpr/ppermute | solution.py:16
  324.1 9.2 %conditional.8 = (bf16[64,2048]{1,0:T(8,128)(2,1)S(1)}, bf16[64,512]{1,0:T(8,128)(2,1)}, bf16[64,512]{0,1:T(8,128)(2,1)}) conditional(s32[]{:T(128)} %convert_element_type.69, () %tuple.79, (bf16[64,1440]{1,0:T(8,128)(2,1)S(1)}, f32[1,1440]{1,0:T(1,128)S(1)}, bf16[1440,2048]{1,0:T(8,128)(2,1)}, f32[64,1,32]{2,0,1:T(8,128)S(1)}, ...), branch_computations={%region_1.1_spmd, %region_2.3_spmd} | conditional | flops 474183744 | bytes 12373788 | solution.py:124
  324.3 3.9 %fusion.26 = f32[64,2048]{1,0:T(8,128)S(1)} fusion(bf16[1440,2048]{1,0:T(8,128)(2,1)} %get-tuple-element.374, bf16[64,1440]{1,0:T(8,128)(2,1)S(1)} %get-tuple-element.372, f32[1440]{0:T(1024)S(1)} %reduce, f32[64]{0:T(128)S(1)} %add_rsqrt_fusion), kind=kOutput, calls=%fused_computation.44 | convolution fusion | flops 377856000 | bytes 6612864 | tf_op jit(solution)/shard_map/while/body/eval_jaxpr/cond/branch_1_fun/dot_general | solution.py:65
  331.7 1.6 copy.18
  333.3 2.3 collective-permute-start
  335.6 1.3 collective-permute-start.1
  338.7 1.5 bitcast_dynamic-update-slice_fusion.5
  340.2 8.0 %conditional.9 = (bf16[64,1440]{1,0:T(8,128)(2,1)S(1)}) conditional(s32[]{:T(128)} %convert_element_type.69, bf16[64,1440]{1,0:T(8,128)(2,1)S(1)} %bitcast_select_fusion.5, (bf16[64,1440]{1,0:T(8,128)(2,1)S(1)}, bf16[64,512]{0,1:T(8,128)(2,1)S(1)}, bf16[64,512]{0,1:T(8,128)(2,1)S(1)}, bf16[64,512]{1,0:T(8,128)(2,1)}, s32[]{:T(128)}, ...), branch_computations={%region_4.4_spmd, %region_5.7_spmd} | conditional | flops 483969664 | bytes 32420688 | solution.py:126
  344.8 1.1 convolution_convert_fusion
  347.0 1.2 fusion.8
  348.2 1.3 collective-permute-start.2
  350.3 6.8 %collective-permute-done.2 = bf16[64,1440]{1,0:T(8,128)(2,1)S(1)} collective-permute-done((bf16[64,1440]{1,0:T(8,128)(2,1)S(1)}, bf16[64,1440]{1,0:T(8,128)(2,1)S(1)}, u32[]{:S(2)}, u32[]{:S(2)}) %collective-permute-start.2) | collective-permute-done | bytes 184352 | tf_op jit(solution)/shard_map/while/body/eval_jaxpr/ppermute | solution.py:16
  (244 shorter events, 75.3 us)
Async XLA Ops:
  7.2 1.4 copy-start.1
  7.2 47.5 %all-gather.3.cloned.1.call-start = ((), (), s32[]{:S(2)}) async-start(), calls=%async_computation | async-start | bytes 7372800 | tf_op jit(solution)/shard_map/all_gather | solution.py:41
  7.9 2.8 copy-start.3
  7.9 94.7 %all-gather.5.cloned.1.call-start = ((), (), s32[]{:S(2)}) async-start(), calls=%async_computation.1 | async-start | bytes 7864320 | tf_op jit(solution)/shard_map/all_gather | solution.py:42
  10.2 94.1 %copy-start = (bf16[1,1440,512]{2,1,0:T(8,128)(2,1)S(1)}, bf16[1,1440,512]{2,1,0:T(8,128)(2,1)}, u32[]{:S(2)}) copy-start(bf16[1,1440,512]{2,1,0:T(8,128)(2,1)} %param.19) | copy-start | bytes 4423684
  10.2 94.1 %copy-start.2 = (f32[1,1440]{1,0:T(1,128)S(1)}, f32[1,1440]{1,0:T(1,128)}, u32[]{:S(2)}) copy-start(f32[1,1440]{1,0:T(1,128)} %param.17) | copy-start | bytes 17284
  10.2 94.1 %copy-start.4 = (s32[4]{0:T(128)S(1)}, s32[4]{0:T(128)}, u32[]{:S(2)}) copy-start(s32[4]{0:T(128)} %param.15) | copy-start | bytes 52
  10.2 94.1 %copy-start.5 = (s32[4]{0:T(128)S(1)}, s32[4]{0:T(128)}, u32[]{:S(2)}) copy-start(s32[4]{0:T(128)} %param.16) | copy-start | bytes 52
  109.1 6.8 %collective-permute-start = (bf16[64,512]{0,1:T(8,128)(2,1)}, bf16[64,512]{0,1:T(8,128)(2,1)S(1)}, u32[]{:S(2)}, u32[]{:S(2)}) collective-permute-start(bf16[64,512]{0,1:T(8,128)(2,1)} %get-tuple-element.696), channel_id=1, source_target_pairs={{0,2},{1,3},{4,6},{5,7},{8,10},{9,11},{12,14},{13,15},{16,18},{17,... | collective-permute-start | bytes 196616 | tf_op jit(solution)/shard_map/while/body/eval_jaxpr/ppermute | solution.py:16
  111.6 4.3 %collective-permute-start.1 = (bf16[64,512]{0,1:T(8,128)(2,1)}, bf16[64,512]{0,1:T(8,128)(2,1)S(1)}, u32[]{:S(2)}, u32[]{:S(2)}) collective-permute-start(bf16[64,512]{0,1:T(8,128)(2,1)} %get-tuple-element.696), channel_id=1, source_target_pairs={{0,1},{1,2},{2,3},{4,5},{5,6},{6,7},{8,9},{9,10},{10,11},{12,13},{... | collective-permute-start | bytes 196616 | tf_op jit(solution)/shard_map/while/body/eval_jaxpr/ppermute | solution.py:16
  116.0 9.3 %collective-permute-start.2 = (bf16[64,1440]{1,0:T(8,128)(2,1)S(1)}, bf16[64,1440]{1,0:T(8,128)(2,1)S(1)}, u32[]{:S(2)}, u32[]{:S(2)}) collective-permute-start(bf16[64,1440]{1,0:T(8,128)(2,1)S(1)} %get-tuple-element.771), channel_id=1, source_target_pairs={{0,4},{4,8},{8,12},{1,5},{5,9},{9,13},{2,6},{6,10},{10,14},{3,7},{... | collective-permute-start | bytes 552968 | tf_op jit(solution)/shard_map/while/body/eval_jaxpr/ppermute | solution.py:16
  130.1 6.8 %collective-permute-start = (bf16[64,512]{0,1:T(8,128)(2,1)}, bf16[64,512]{0,1:T(8,128)(2,1)S(1)}, u32[]{:S(2)}, u32[]{:S(2)}) collective-permute-start(bf16[64,512]{0,1:T(8,128)(2,1)} %get-tuple-element.696), channel_id=1, source_target_pairs={{0,2},{1,3},{4,6},{5,7},{8,10},{9,11},{12,14},{13,15},{16,18},{17,... | collective-permute-start | bytes 196616 | tf_op jit(solution)/shard_map/while/body/eval_jaxpr/ppermute | solution.py:16
  133.2 3.8 %collective-permute-start.1 = (bf16[64,512]{0,1:T(8,128)(2,1)}, bf16[64,512]{0,1:T(8,128)(2,1)S(1)}, u32[]{:S(2)}, u32[]{:S(2)}) collective-permute-start(bf16[64,512]{0,1:T(8,128)(2,1)} %get-tuple-element.696), channel_id=1, source_target_pairs={{0,1},{1,2},{2,3},{4,5},{5,6},{6,7},{8,9},{9,10},{10,11},{12,13},{... | collective-permute-start | bytes 196616 | tf_op jit(solution)/shard_map/while/body/eval_jaxpr/ppermute | solution.py:16
  137.0 9.2 %collective-permute-start.2 = (bf16[64,1440]{1,0:T(8,128)(2,1)S(1)}, bf16[64,1440]{1,0:T(8,128)(2,1)S(1)}, u32[]{:S(2)}, u32[]{:S(2)}) collective-permute-start(bf16[64,1440]{1,0:T(8,128)(2,1)S(1)} %get-tuple-element.771), channel_id=1, source_target_pairs={{0,4},{4,8},{8,12},{1,5},{5,9},{9,13},{2,6},{6,10},{10,14},{3,7},{... | collective-permute-start | bytes 552968 | tf_op jit(solution)/shard_map/while/body/eval_jaxpr/ppermute | solution.py:16
  151.0 6.8 %collective-permute-start = (bf16[64,512]{0,1:T(8,128)(2,1)}, bf16[64,512]{0,1:T(8,128)(2,1)S(1)}, u32[]{:S(2)}, u32[]{:S(2)}) collective-permute-start(bf16[64,512]{0,1:T(8,128)(2,1)} %get-tuple-element.696), channel_id=1, source_target_pairs={{0,2},{1,3},{4,6},{5,7},{8,10},{9,11},{12,14},{13,15},{16,18},{17,... | collective-permute-start | bytes 196616 | tf_op jit(solution)/shard_map/while/body/eval_jaxpr/ppermute | solution.py:16
  154.0 3.8 %collective-permute-start.1 = (bf16[64,512]{0,1:T(8,128)(2,1)}, bf16[64,512]{0,1:T(8,128)(2,1)S(1)}, u32[]{:S(2)}, u32[]{:S(2)}) collective-permute-start(bf16[64,512]{0,1:T(8,128)(2,1)} %get-tuple-element.696), channel_id=1, source_target_pairs={{0,1},{1,2},{2,3},{4,5},{5,6},{6,7},{8,9},{9,10},{10,11},{12,13},{... | collective-permute-start | bytes 196616 | tf_op jit(solution)/shard_map/while/body/eval_jaxpr/ppermute | solution.py:16
  157.8 52.5 %collective-permute-start.2 = (bf16[64,1440]{1,0:T(8,128)(2,1)S(1)}, bf16[64,1440]{1,0:T(8,128)(2,1)S(1)}, u32[]{:S(2)}, u32[]{:S(2)}) collective-permute-start(bf16[64,1440]{1,0:T(8,128)(2,1)S(1)} %get-tuple-element.771), channel_id=1, source_target_pairs={{0,4},{4,8},{8,12},{1,5},{5,9},{9,13},{2,6},{6,10},{10,14},{3,7},{... | collective-permute-start | bytes 552968 | tf_op jit(solution)/shard_map/while/body/eval_jaxpr/ppermute | solution.py:16
  223.0 6.9 %collective-permute-start = (bf16[64,512]{0,1:T(8,128)(2,1)}, bf16[64,512]{0,1:T(8,128)(2,1)S(1)}, u32[]{:S(2)}, u32[]{:S(2)}) collective-permute-start(bf16[64,512]{0,1:T(8,128)(2,1)} %get-tuple-element.696), channel_id=1, source_target_pairs={{0,2},{1,3},{4,6},{5,7},{8,10},{9,11},{12,14},{13,15},{16,18},{17,... | collective-permute-start | bytes 196616 | tf_op jit(solution)/shard_map/while/body/eval_jaxpr/ppermute | solution.py:16
  225.4 4.6 %collective-permute-start.1 = (bf16[64,512]{0,1:T(8,128)(2,1)}, bf16[64,512]{0,1:T(8,128)(2,1)S(1)}, u32[]{:S(2)}, u32[]{:S(2)}) collective-permute-start(bf16[64,512]{0,1:T(8,128)(2,1)} %get-tuple-element.696), channel_id=1, source_target_pairs={{0,1},{1,2},{2,3},{4,5},{5,6},{6,7},{8,9},{9,10},{10,11},{12,13},{... | collective-permute-start | bytes 196616 | tf_op jit(solution)/shard_map/while/body/eval_jaxpr/ppermute | solution.py:16
  233.7 2.2 slice-start
  234.5 2.2 slice-start.1
  238.0 9.1 %collective-permute-start.2 = (bf16[64,1440]{1,0:T(8,128)(2,1)S(1)}, bf16[64,1440]{1,0:T(8,128)(2,1)S(1)}, u32[]{:S(2)}, u32[]{:S(2)}) collective-permute-start(bf16[64,1440]{1,0:T(8,128)(2,1)S(1)} %get-tuple-element.771), channel_id=1, source_target_pairs={{0,4},{4,8},{8,12},{1,5},{5,9},{9,13},{2,6},{6,10},{10,14},{3,7},{... | collective-permute-start | bytes 552968 | tf_op jit(solution)/shard_map/while/body/eval_jaxpr/ppermute | solution.py:16
  259.8 6.9 %collective-permute-start = (bf16[64,512]{0,1:T(8,128)(2,1)}, bf16[64,512]{0,1:T(8,128)(2,1)S(1)}, u32[]{:S(2)}, u32[]{:S(2)}) collective-permute-start(bf16[64,512]{0,1:T(8,128)(2,1)} %get-tuple-element.696), channel_id=1, source_target_pairs={{0,2},{1,3},{4,6},{5,7},{8,10},{9,11},{12,14},{13,15},{16,18},{17,... | collective-permute-start | bytes 196616 | tf_op jit(solution)/shard_map/while/body/eval_jaxpr/ppermute | solution.py:16
  262.1 4.6 %collective-permute-start.1 = (bf16[64,512]{0,1:T(8,128)(2,1)}, bf16[64,512]{0,1:T(8,128)(2,1)S(1)}, u32[]{:S(2)}, u32[]{:S(2)}) collective-permute-start(bf16[64,512]{0,1:T(8,128)(2,1)} %get-tuple-element.696), channel_id=1, source_target_pairs={{0,1},{1,2},{2,3},{4,5},{5,6},{6,7},{8,9},{9,10},{10,11},{12,13},{... | collective-permute-start | bytes 196616 | tf_op jit(solution)/shard_map/while/body/eval_jaxpr/ppermute | solution.py:16
  270.4 2.2 slice-start
  271.3 2.2 slice-start.1
  274.7 9.1 %collective-permute-start.2 = (bf16[64,1440]{1,0:T(8,128)(2,1)S(1)}, bf16[64,1440]{1,0:T(8,128)(2,1)S(1)}, u32[]{:S(2)}, u32[]{:S(2)}) collective-permute-start(bf16[64,1440]{1,0:T(8,128)(2,1)S(1)} %get-tuple-element.771), channel_id=1, source_target_pairs={{0,4},{4,8},{8,12},{1,5},{5,9},{9,13},{2,6},{6,10},{10,14},{3,7},{... | collective-permute-start | bytes 552968 | tf_op jit(solution)/shard_map/while/body/eval_jaxpr/ppermute | solution.py:16
  296.5 6.9 %collective-permute-start = (bf16[64,512]{0,1:T(8,128)(2,1)}, bf16[64,512]{0,1:T(8,128)(2,1)S(1)}, u32[]{:S(2)}, u32[]{:S(2)}) collective-permute-start(bf16[64,512]{0,1:T(8,128)(2,1)} %get-tuple-element.696), channel_id=1, source_target_pairs={{0,2},{1,3},{4,6},{5,7},{8,10},{9,11},{12,14},{13,15},{16,18},{17,... | collective-permute-start | bytes 196616 | tf_op jit(solution)/shard_map/while/body/eval_jaxpr/ppermute | solution.py:16
  298.9 4.6 %collective-permute-start.1 = (bf16[64,512]{0,1:T(8,128)(2,1)}, bf16[64,512]{0,1:T(8,128)(2,1)S(1)}, u32[]{:S(2)}, u32[]{:S(2)}) collective-permute-start(bf16[64,512]{0,1:T(8,128)(2,1)} %get-tuple-element.696), channel_id=1, source_target_pairs={{0,1},{1,2},{2,3},{4,5},{5,6},{6,7},{8,9},{9,10},{10,11},{12,13},{... | collective-permute-start | bytes 196616 | tf_op jit(solution)/shard_map/while/body/eval_jaxpr/ppermute | solution.py:16
  307.1 2.2 slice-start
  308.0 2.2 slice-start.1
  311.5 9.1 %collective-permute-start.2 = (bf16[64,1440]{1,0:T(8,128)(2,1)S(1)}, bf16[64,1440]{1,0:T(8,128)(2,1)S(1)}, u32[]{:S(2)}, u32[]{:S(2)}) collective-permute-start(bf16[64,1440]{1,0:T(8,128)(2,1)S(1)} %get-tuple-element.771), channel_id=1, source_target_pairs={{0,4},{4,8},{8,12},{1,5},{5,9},{9,13},{2,6},{6,10},{10,14},{3,7},{... | collective-permute-start | bytes 552968 | tf_op jit(solution)/shard_map/while/body/eval_jaxpr/ppermute | solution.py:16
  333.3 6.9 %collective-permute-start = (bf16[64,512]{0,1:T(8,128)(2,1)}, bf16[64,512]{0,1:T(8,128)(2,1)S(1)}, u32[]{:S(2)}, u32[]{:S(2)}) collective-permute-start(bf16[64,512]{0,1:T(8,128)(2,1)} %get-tuple-element.696), channel_id=1, source_target_pairs={{0,2},{1,3},{4,6},{5,7},{8,10},{9,11},{12,14},{13,15},{16,18},{17,... | collective-permute-start | bytes 196616 | tf_op jit(solution)/shard_map/while/body/eval_jaxpr/ppermute | solution.py:16
  335.6 4.6 %collective-permute-start.1 = (bf16[64,512]{0,1:T(8,128)(2,1)}, bf16[64,512]{0,1:T(8,128)(2,1)S(1)}, u32[]{:S(2)}, u32[]{:S(2)}) collective-permute-start(bf16[64,512]{0,1:T(8,128)(2,1)} %get-tuple-element.696), channel_id=1, source_target_pairs={{0,1},{1,2},{2,3},{4,5},{5,6},{6,7},{8,9},{9,10},{10,11},{12,13},{... | collective-permute-start | bytes 196616 | tf_op jit(solution)/shard_map/while/body/eval_jaxpr/ppermute | solution.py:16
  343.9 2.2 slice-start
  344.8 2.2 slice-start.1
  348.2 8.8 %collective-permute-start.2 = (bf16[64,1440]{1,0:T(8,128)(2,1)S(1)}, bf16[64,1440]{1,0:T(8,128)(2,1)S(1)}, u32[]{:S(2)}, u32[]{:S(2)}) collective-permute-start(bf16[64,1440]{1,0:T(8,128)(2,1)S(1)} %get-tuple-element.771), channel_id=1, source_target_pairs={{0,4},{4,8},{8,12},{1,5},{5,9},{9,13},{2,6},{6,10},{10,14},{3,7},{... | collective-permute-start | bytes 552968 | tf_op jit(solution)/shard_map/while/body/eval_jaxpr/ppermute | solution.py:16
Sparse Core Ops, SparseCore 0:
  9.5 45.0 all-gather.2
  56.2 46.3 all-gather.4
where the time goes:
time: 366 us; the launch traced here: 364 us
  waiting for transfers between devices  185 us (51%)
  local copies, waits for them, and re-layouts  49.8 us (14%)
  starting transfers between devices  36.5 us (10%)
  other arithmetic  35.7 us (10%)
  matrix products  28.7 us (8%)
  loops' own time  14.3 us (4%)
  between operations  14.1 us (4%)
    ppermute x21, waiting for transfers between devices, from_behind(): return lax.ppermute(block, axis, route)  92.9 us
    all_gather x1, waiting for transfers between devices, per_device(): lax.all_gather(w_out, 'seq', axis=1, tiled=True)  47.9 us
    all_gather x1, waiting for transfers between devices, per_device(): lax.all_gather(w_query, 'seq', axis=2, tiled=True)  43.2 us
    ppermute x21, starting transfers between devices, from_behind(): return lax.ppermute(block, axis, route)  36.5 us
    dot_general x4, matrix products, project(): jnp.dot(normed, query_weight, preferred_element_type=jnp.float32)  15.5 us
    another operation x1, loops' own time, per_device(): final = lax.fori_loop(0, micro + sections - 1, turn, initial)  13.4 us
    dynamic_update_slice x7, other arithmetic, turn(): lax.dynamic_update_index_in_dim(cache_buffer, jnp.where(active, cache, pr...  7.9 us
    another operation x13, local copies, waits for them, and re-layouts  7.83 us
  transfers between devices with their start and end apart: 23, of which 9 were waited for; matrix products, arithmetic and copies ran while one was open for 8% of the time, Pallas kernels for 0%

commit v1 on v0

--- a/solution.py
+++ b/solution.py
@@ -38,7 +38,7 @@
     seq_index = lax.axis_index("seq")
     micro, rows, width = tokens.shape
     full_query, full_out = (
-        lax.all_gather(w_query, "seq", axis=2, tiled=True),
+        jnp.concatenate(lax.all_gather(w_query, "seq"), axis=2),
         lax.all_gather(w_out, "seq", axis=1, tiled=True),
     )
     query_weight = full_query[0]

time: 366 us -> 366 us (level)
  waiting for transfers between devices: 185 us -> 159 us
  local copies, waits for them, and re-layouts: 49.8 us -> 75.5 us
    all_gather x1, waiting for transfers between devices: 47.9 us -> 22.3 us  [per_device(): lax.all_gather(w_out, 'seq', axis=1, tiled=True)]
    reshape x0 -> x1, local copies, waits for them, and re-layouts: none -> 20.6 us  [per_device(): jnp.concatenate(lax.all_gather(w_query, 'seq'), axis=2)]
    unnamed x14 -> x15, local copies, waits for them, and re-layouts: 2.72 us -> 7.81 us
  transfers between devices with their start and end apart: 23 -> 23, of which waited for: 9 -> 9; matrix products, arithmetic and copies ran while one was open for 8% -> 15% of each run, Pallas kernels for 0% -> 0%
where the time goes in v1:
time: 366 us; the launch traced here: 364 us
  waiting for transfers between devices  159 us (43%)
  local copies, waits for them, and re-layouts  75.5 us (21%)
  starting transfers between devices  36.5 us (10%)
  other arithmetic  35.7 us (10%)
  matrix products  28.7 us (8%)
  loops' own time  14.5 us (4%)
  between operations  14.1 us (4%)
    ppermute x21, waiting for transfers between devices, from_behind(): return lax.ppermute(block, axis, route)  92.9 us
    all_gather x1, waiting for transfers between devices, per_device(): lax.all_gather(w_query, 'seq')  43.2 us
    ppermute x21, starting transfers between devices, from_behind(): return lax.ppermute(block, axis, route)  36.5 us
    all_gather x1, waiting for transfers between devices, per_device(): lax.all_gather(w_out, 'seq', axis=1, tiled=True)  22.3 us
    reshape x1, local copies, waits for them, and re-layouts, per_device(): jnp.concatenate(lax.all_gather(w_query, 'seq'), axis=2)  20.6 us
    dot_general x4, matrix products, project(): jnp.dot(normed, query_weight, preferred_element_type=jnp.float32)  15.5 us
    another operation x1, loops' own time, per_device(): final = lax.fori_loop(0, micro + sections - 1, turn, initial)  13.6 us
    dynamic_update_slice x7, other arithmetic, turn(): lax.dynamic_update_index_in_dim(cache_buffer, jnp.where(active, cache, pr...  7.9 us
  transfers between devices with their start and end apart: 23, of which 9 were waited for; matrix products, arithmetic and copies ran while one was open for 15% of the time, Pallas kernels for 0%

profile of v1, /device:TPU:28, one launch (start us, length us, event | category | flops | bytes accessed | tf_op | source)
XLA Modules:
  0.0 364.1 jit_solution(291645818742250799)
XLA Ops:
  8.5 1.6 copy.26
  11.5 43.2 %all-gather.6.cloned.1.call-done = bf16[4,1440,512]{2,1,0:T(8,128)(2,1)} async-done(((bf16[1,1440,512]{2,1,0:T(8,128)(2,1)}), bf16[4,1440,512]{2,1,0:T(8,128)(2,1)}) %all-gather.6.cloned.1.call-update) | async-done | bytes 5898256 | tf_op jit(solution)/shard_map/all_gather | solution.py:41
  54.6 20.6 %copy.25 = bf16[1,1440,4,512]{3,2,1,0:T(4,128)(2,1)S(1)} copy(bf16[1,1440,4,512]{3,1,2,0:T(8,128)(2,1)} %bitcast.84) | data formatting | bytes 11796480 | tf_op jit(solution)/shard_map/reshape | solution.py:41
  75.2 5.1 %copy.31 = bf16[180,8,4,512]{3,1,2,0:T(8,128)(2,1)} copy(bf16[180,8,4,512]{3,2,1,0:T(4,128)(2,1)S(1)} %bitcast.81) | data formatting | bytes 11796480
  80.3 22.3 %all-gather.4.cloned.1.call-done = bf16[1,2048,1440]{2,1,0:T(8,128)(2,1)} async-done(((bf16[1,512,1440]{2,1,0:T(8,128)(2,1)}), bf16[1,2048,1440]{2,1,0:T(8,128)(2,1)}) %all-gather.4.cloned.1.call-update) | async-done | bytes 5898256 | tf_op jit(solution)/shard_map/all_gather | solution.py:42
  104.3 252.9 %while.20 = (s32[]{:T(128)}, bf16[64,1440]{1,0:T(8,128)(2,1)S(1)}, bf16[4,64,1440]{2,1,0:T(8,128)(2,1)}, bf16[4,64,512]{2,1,0:T(8,128)(2,1)}, s32[]{:T(128)}, /*...) while((s32[]{:T(128)}, bf16[64,1440]{1,0:T(8,128)(2,1)S(1)}, ...), condition=%wide.region_8.9_spmd.clone.clone, body=%wide.region_0.8_spmd.clone.clone.sunk | while | flops 958372544 | bytes 47880768 | solution.py:143
  108.0 1.4 conditional.8
  109.3 2.5 collective-permute-start
  111.8 1.9 collective-permute-start.1
  116.2 1.3 collective-permute-start.2
  118.2 7.3 %collective-permute-done.2 = bf16[64,1440]{1,0:T(8,128)(2,1)S(1)} collective-permute-done((bf16[64,1440]{1,0:T(8,128)(2,1)S(1)}, bf16[64,1440]{1,0:T(8,128)(2,1)S(1)}, u32[]{:S(2)}, u32[]{:S(2)}) %collective-permute-start.2) | collective-permute-done | bytes 184352 | tf_op jit(solution)/shard_map/while/body/eval_jaxpr/ppermute | solution.py:16
  129.0 1.4 conditional.8
  130.3 3.0 collective-permute-start
  133.3 1.3 collective-permute-start.1
  137.1 1.3 collective-permute-start.2
  139.2 7.2 %collective-permute-done.2 = bf16[64,1440]{1,0:T(8,128)(2,1)S(1)} collective-permute-done((bf16[64,1440]{1,0:T(8,128)(2,1)S(1)}, bf16[64,1440]{1,0:T(8,128)(2,1)S(1)}, u32[]{:S(2)}, u32[]{:S(2)}) %collective-permute-start.2) | collective-permute-done | bytes 184352 | tf_op jit(solution)/shard_map/while/body/eval_jaxpr/ppermute | solution.py:16
  149.8 1.4 conditional.8
  151.2 3.0 collective-permute-start
  154.2 1.3 collective-permute-start.1
  158.0 1.3 collective-permute-start.2
  160.0 50.5 %collective-permute-done.2 = bf16[64,1440]{1,0:T(8,128)(2,1)S(1)} collective-permute-done((bf16[64,1440]{1,0:T(8,128)(2,1)S(1)}, bf16[64,1440]{1,0:T(8,128)(2,1)S(1)}, u32[]{:S(2)}, u32[]{:S(2)}) %collective-permute-start.2) | collective-permute-done | bytes 184352 | tf_op jit(solution)/shard_map/while/body/eval_jaxpr/ppermute | solution.py:16
  214.0 9.2 %conditional.8 = (bf16[64,2048]{1,0:T(8,128)(2,1)S(1)}, bf16[64,512]{1,0:T(8,128)(2,1)}, bf16[64,512]{0,1:T(8,128)(2,1)}) conditional(s32[]{:T(128)} %convert_element_type.69, () %tuple.81, (bf16[64,1440]{1,0:T(8,128)(2,1)S(1)}, f32[1,1440]{1,0:T(1,128)S(1)}, bf16[1440,2048]{1,0:T(8,128)(2,1)}, f32[64,1,32]{2,0,1:T(8,128)S(1)}, ...), branch_computations={%region_1.1_spmd, %region_2.3_spmd} | conditional | flops 474183744 | bytes 12373788 | solution.py:124
  214.2 3.9 %fusion.26 = f32[64,2048]{1,0:T(8,128)S(1)} fusion(bf16[1440,2048]{1,0:T(8,128)(2,1)} %get-tuple-element.374, bf16[64,1440]{1,0:T(8,128)(2,1)S(1)} %get-tuple-element.372, f32[1440]{0:T(1024)S(1)} %reduce, f32[64]{0:T(128)S(1)} %add_rsqrt_fusion), kind=kOutput, calls=%fused_computation.44 | convolution fusion | flops 377856000 | bytes 6612864 | tf_op jit(solution)/shard_map/while/body/eval_jaxpr/cond/branch_1_fun/dot_general | solution.py:65
  221.6 1.6 copy.30
  223.2 2.3 collective-permute-start
  225.5 1.3 collective-permute-start.1
  228.6 1.5 bitcast_dynamic-update-slice_fusion.5
  230.1 8.0 %conditional.9 = (bf16[64,1440]{1,0:T(8,128)(2,1)S(1)}) conditional(s32[]{:T(128)} %convert_element_type.69, bf16[64,1440]{1,0:T(8,128)(2,1)S(1)} %bitcast_select_fusion.5, (bf16[64,1440]{1,0:T(8,128)(2,1)S(1)}, bf16[64,512]{0,1:T(8,128)(2,1)S(1)}, bf16[64,512]{0,1:T(8,128)(2,1)S(1)}, bf16[64,512]{1,0:T(8,128)(2,1)}, s32[]{:T(128)}, ...), branch_computations={%region_4.4_spmd, %region_5.7_spmd} | conditional | flops 483969664 | bytes 32420688 | solution.py:126
  234.7 1.1 convolution_convert_fusion
  236.9 1.2 fusion.8
  238.2 1.3 collective-permute-start.2
  240.2 7.1 %collective-permute-done.2 = bf16[64,1440]{1,0:T(8,128)(2,1)S(1)} collective-permute-done((bf16[64,1440]{1,0:T(8,128)(2,1)S(1)}, bf16[64,1440]{1,0:T(8,128)(2,1)S(1)}, u32[]{:S(2)}, u32[]{:S(2)}) %collective-permute-start.2) | collective-permute-done | bytes 184352 | tf_op jit(solution)/shard_map/while/body/eval_jaxpr/ppermute | solution.py:16
  250.7 9.2 %conditional.8 = (bf16[64,2048]{1,0:T(8,128)(2,1)S(1)}, bf16[64,512]{1,0:T(8,128)(2,1)}, bf16[64,512]{0,1:T(8,128)(2,1)}) conditional(s32[]{:T(128)} %convert_element_type.69, () %tuple.81, (bf16[64,1440]{1,0:T(8,128)(2,1)S(1)}, f32[1,1440]{1,0:T(1,128)S(1)}, bf16[1440,2048]{1,0:T(8,128)(2,1)}, f32[64,1,32]{2,0,1:T(8,128)S(1)}, ...), branch_computations={%region_1.1_spmd, %region_2.3_spmd} | conditional | flops 474183744 | bytes 12373788 | solution.py:124
  250.9 3.9 %fusion.26 = f32[64,2048]{1,0:T(8,128)S(1)} fusion(bf16[1440,2048]{1,0:T(8,128)(2,1)} %get-tuple-element.374, bf16[64,1440]{1,0:T(8,128)(2,1)S(1)} %get-tuple-element.372, f32[1440]{0:T(1024)S(1)} %reduce, f32[64]{0:T(128)S(1)} %add_rsqrt_fusion), kind=kOutput, calls=%fused_computation.44 | convolution fusion | flops 377856000 | bytes 6612864 | tf_op jit(solution)/shard_map/while/body/eval_jaxpr/cond/branch_1_fun/dot_general | solution.py:65
  258.4 1.6 copy.30
  260.0 2.3 collective-permute-start
  262.3 1.3 collective-permute-start.1
  265.4 1.5 bitcast_dynamic-update-slice_fusion.5
  266.9 8.0 %conditional.9 = (bf16[64,1440]{1,0:T(8,128)(2,1)S(1)}) conditional(s32[]{:T(128)} %convert_element_type.69, bf16[64,1440]{1,0:T(8,128)(2,1)S(1)} %bitcast_select_fusion.5, (bf16[64,1440]{1,0:T(8,128)(2,1)S(1)}, bf16[64,512]{0,1:T(8,128)(2,1)S(1)}, bf16[64,512]{0,1:T(8,128)(2,1)S(1)}, bf16[64,512]{1,0:T(8,128)(2,1)}, s32[]{:T(128)}, ...), branch_computations={%region_4.4_spmd, %region_5.7_spmd} | conditional | flops 483969664 | bytes 32420688 | solution.py:126
  271.5 1.1 convolution_convert_fusion
  273.7 1.2 fusion.8
  274.9 1.3 collective-permute-start.2
  276.9 7.1 %collective-permute-done.2 = bf16[64,1440]{1,0:T(8,128)(2,1)S(1)} collective-permute-done((bf16[64,1440]{1,0:T(8,128)(2,1)S(1)}, bf16[64,1440]{1,0:T(8,128)(2,1)S(1)}, u32[]{:S(2)}, u32[]{:S(2)}) %collective-permute-start.2) | collective-permute-done | bytes 184352 | tf_op jit(solution)/shard_map/while/body/eval_jaxpr/ppermute | solution.py:16
  287.5 9.2 %conditional.8 = (bf16[64,2048]{1,0:T(8,128)(2,1)S(1)}, bf16[64,512]{1,0:T(8,128)(2,1)}, bf16[64,512]{0,1:T(8,128)(2,1)}) conditional(s32[]{:T(128)} %convert_element_type.69, () %tuple.81, (bf16[64,1440]{1,0:T(8,128)(2,1)S(1)}, f32[1,1440]{1,0:T(1,128)S(1)}, bf16[1440,2048]{1,0:T(8,128)(2,1)}, f32[64,1,32]{2,0,1:T(8,128)S(1)}, ...), branch_computations={%region_1.1_spmd, %region_2.3_spmd} | conditional | flops 474183744 | bytes 12373788 | solution.py:124
  287.7 3.9 %fusion.26 = f32[64,2048]{1,0:T(8,128)S(1)} fusion(bf16[1440,2048]{1,0:T(8,128)(2,1)} %get-tuple-element.374, bf16[64,1440]{1,0:T(8,128)(2,1)S(1)} %get-tuple-element.372, f32[1440]{0:T(1024)S(1)} %reduce, f32[64]{0:T(128)S(1)} %add_rsqrt_fusion), kind=kOutput, calls=%fused_computation.44 | convolution fusion | flops 377856000 | bytes 6612864 | tf_op jit(solution)/shard_map/while/body/eval_jaxpr/cond/branch_1_fun/dot_general | solution.py:65
  295.1 1.6 copy.30
  296.7 2.3 collective-permute-start
  299.0 1.3 collective-permute-start.1
  302.1 1.5 bitcast_dynamic-update-slice_fusion.5
  303.6 8.0 %conditional.9 = (bf16[64,1440]{1,0:T(8,128)(2,1)S(1)}) conditional(s32[]{:T(128)} %convert_element_type.69, bf16[64,1440]{1,0:T(8,128)(2,1)S(1)} %bitcast_select_fusion.5, (bf16[64,1440]{1,0:T(8,128)(2,1)S(1)}, bf16[64,512]{0,1:T(8,128)(2,1)S(1)}, bf16[64,512]{0,1:T(8,128)(2,1)S(1)}, bf16[64,512]{1,0:T(8,128)(2,1)}, s32[]{:T(128)}, ...), branch_computations={%region_4.4_spmd, %region_5.7_spmd} | conditional | flops 483969664 | bytes 32420688 | solution.py:126
  310.4 1.2 fusion.8
  311.7 1.3 collective-permute-start.2
  313.7 7.1 %collective-permute-done.2 = bf16[64,1440]{1,0:T(8,128)(2,1)S(1)} collective-permute-done((bf16[64,1440]{1,0:T(8,128)(2,1)S(1)}, bf16[64,1440]{1,0:T(8,128)(2,1)S(1)}, u32[]{:S(2)}, u32[]{:S(2)}) %collective-permute-start.2) | collective-permute-done | bytes 184352 | tf_op jit(solution)/shard_map/while/body/eval_jaxpr/ppermute | solution.py:16
  324.2 9.2 %conditional.8 = (bf16[64,2048]{1,0:T(8,128)(2,1)S(1)}, bf16[64,512]{1,0:T(8,128)(2,1)}, bf16[64,512]{0,1:T(8,128)(2,1)}) conditional(s32[]{:T(128)} %convert_element_type.69, () %tuple.81, (bf16[64,1440]{1,0:T(8,128)(2,1)S(1)}, f32[1,1440]{1,0:T(1,128)S(1)}, bf16[1440,2048]{1,0:T(8,128)(2,1)}, f32[64,1,32]{2,0,1:T(8,128)S(1)}, ...), branch_computations={%region_1.1_spmd, %region_2.3_spmd} | conditional | flops 474183744 | bytes 12373788 | solution.py:124
  324.4 3.9 %fusion.26 = f32[64,2048]{1,0:T(8,128)S(1)} fusion(bf16[1440,2048]{1,0:T(8,128)(2,1)} %get-tuple-element.374, bf16[64,1440]{1,0:T(8,128)(2,1)S(1)} %get-tuple-element.372, f32[1440]{0:T(1024)S(1)} %reduce, f32[64]{0:T(128)S(1)} %add_rsqrt_fusion), kind=kOutput, calls=%fused_computation.44 | convolution fusion | flops 377856000 | bytes 6612864 | tf_op jit(solution)/shard_map/while/body/eval_jaxpr/cond/branch_1_fun/dot_general | solution.py:65
  331.9 1.6 copy.30
  333.5 2.3 collective-permute-start
  335.8 1.3 collective-permute-start.1
  338.9 1.5 bitcast_dynamic-update-slice_fusion.5
  340.4 8.0 %conditional.9 = (bf16[64,1440]{1,0:T(8,128)(2,1)S(1)}) conditional(s32[]{:T(128)} %convert_element_type.69, bf16[64,1440]{1,0:T(8,128)(2,1)S(1)} %bitcast_select_fusion.5, (bf16[64,1440]{1,0:T(8,128)(2,1)S(1)}, bf16[64,512]{0,1:T(8,128)(2,1)S(1)}, bf16[64,512]{0,1:T(8,128)(2,1)S(1)}, bf16[64,512]{1,0:T(8,128)(2,1)}, s32[]{:T(128)}, ...), branch_computations={%region_4.4_spmd, %region_5.7_spmd} | conditional | flops 483969664 | bytes 32420688 | solution.py:126
  345.0 1.1 convolution_convert_fusion
  347.2 1.2 fusion.8
  348.4 1.3 collective-permute-start.2
  350.4 6.8 %collective-permute-done.2 = bf16[64,1440]{1,0:T(8,128)(2,1)S(1)} collective-permute-done((bf16[64,1440]{1,0:T(8,128)(2,1)S(1)}, bf16[64,1440]{1,0:T(8,128)(2,1)S(1)}, u32[]{:S(2)}, u32[]{:S(2)}) %collective-permute-start.2) | collective-permute-done | bytes 184352 | tf_op jit(solution)/shard_map/while/body/eval_jaxpr/ppermute | solution.py:16
  (246 shorter events, 77.4 us)
Async XLA Ops:
  7.2 1.4 copy-start.1
  7.2 47.5 %all-gather.6.cloned.1.call-start = ((), (), s32[]{:S(2)}) async-start(), calls=%async_computation.1 | async-start | bytes 7372800 | tf_op jit(solution)/shard_map/all_gather | solution.py:41
  7.9 2.8 copy-start.3
  7.9 94.7 %all-gather.4.cloned.1.call-start = ((), (), s32[]{:S(2)}) async-start(), calls=%async_computation | async-start | bytes 7864320 | tf_op jit(solution)/shard_map/all_gather | solution.py:42
  75.2 29.1 %copy-start = (bf16[1,1440,512]{2,1,0:T(8,128)(2,1)S(1)}, bf16[1,1440,512]{2,1,0:T(8,128)(2,1)}, u32[]{:S(2)}) copy-start(bf16[1,1440,512]{2,1,0:T(8,128)(2,1)} %param.19) | copy-start | bytes 4423684
  75.2 29.1 %copy-start.2 = (f32[1,1440]{1,0:T(1,128)S(1)}, f32[1,1440]{1,0:T(1,128)}, u32[]{:S(2)}) copy-start(f32[1,1440]{1,0:T(1,128)} %param.17) | copy-start | bytes 17284
  75.2 29.1 %copy-start.4 = (s32[4]{0:T(128)S(1)}, s32[4]{0:T(128)}, u32[]{:S(2)}) copy-start(s32[4]{0:T(128)} %param.15) | copy-start | bytes 52
  75.2 29.0 %copy-start.5 = (s32[4]{0:T(128)S(1)}, s32[4]{0:T(128)}, u32[]{:S(2)}) copy-start(s32[4]{0:T(128)} %param.16) | copy-start | bytes 52
  109.3 6.8 %collective-permute-start = (bf16[64,512]{0,1:T(8,128)(2,1)}, bf16[64,512]{0,1:T(8,128)(2,1)S(1)}, u32[]{:S(2)}, u32[]{:S(2)}) collective-permute-start(bf16[64,512]{0,1:T(8,128)(2,1)} %get-tuple-element.718), channel_id=1, source_target_pairs={{0,2},{1,3},{4,6},{5,7},{8,10},{9,11},{12,14},{13,15},{16,18},{17,... | collective-permute-start | bytes 196616 | tf_op jit(solution)/shard_map/while/body/eval_jaxpr/ppermute | solution.py:16
  111.8 4.3 %collective-permute-start.1 = (bf16[64,512]{0,1:T(8,128)(2,1)}, bf16[64,512]{0,1:T(8,128)(2,1)S(1)}, u32[]{:S(2)}, u32[]{:S(2)}) collective-permute-start(bf16[64,512]{0,1:T(8,128)(2,1)} %get-tuple-element.718), channel_id=1, source_target_pairs={{0,1},{1,2},{2,3},{4,5},{5,6},{6,7},{8,9},{9,10},{10,11},{12,13},{... | collective-permute-start | bytes 196616 | tf_op jit(solution)/shard_map/while/body/eval_jaxpr/ppermute | solution.py:16
  116.2 9.3 %collective-permute-start.2 = (bf16[64,1440]{1,0:T(8,128)(2,1)S(1)}, bf16[64,1440]{1,0:T(8,128)(2,1)S(1)}, u32[]{:S(2)}, u32[]{:S(2)}) collective-permute-start(bf16[64,1440]{1,0:T(8,128)(2,1)S(1)} %get-tuple-element.793), channel_id=1, source_target_pairs={{0,4},{4,8},{8,12},{1,5},{5,9},{9,13},{2,6},{6,10},{10,14},{3,7},{... | collective-permute-start | bytes 552968 | tf_op jit(solution)/shard_map/while/body/eval_jaxpr/ppermute | solution.py:16
  130.3 6.8 %collective-permute-start = (bf16[64,512]{0,1:T(8,128)(2,1)}, bf16[64,512]{0,1:T(8,128)(2,1)S(1)}, u32[]{:S(2)}, u32[]{:S(2)}) collective-permute-start(bf16[64,512]{0,1:T(8,128)(2,1)} %get-tuple-element.718), channel_id=1, source_target_pairs={{0,2},{1,3},{4,6},{5,7},{8,10},{9,11},{12,14},{13,15},{16,18},{17,... | collective-permute-start | bytes 196616 | tf_op jit(solution)/shard_map/while/body/eval_jaxpr/ppermute | solution.py:16
  133.3 3.8 %collective-permute-start.1 = (bf16[64,512]{0,1:T(8,128)(2,1)}, bf16[64,512]{0,1:T(8,128)(2,1)S(1)}, u32[]{:S(2)}, u32[]{:S(2)}) collective-permute-start(bf16[64,512]{0,1:T(8,128)(2,1)} %get-tuple-element.718), channel_id=1, source_target_pairs={{0,1},{1,2},{2,3},{4,5},{5,6},{6,7},{8,9},{9,10},{10,11},{12,13},{... | collective-permute-start | bytes 196616 | tf_op jit(solution)/shard_map/while/body/eval_jaxpr/ppermute | solution.py:16
  137.1 9.2 %collective-permute-start.2 = (bf16[64,1440]{1,0:T(8,128)(2,1)S(1)}, bf16[64,1440]{1,0:T(8,128)(2,1)S(1)}, u32[]{:S(2)}, u32[]{:S(2)}) collective-permute-start(bf16[64,1440]{1,0:T(8,128)(2,1)S(1)} %get-tuple-element.793), channel_id=1, source_target_pairs={{0,4},{4,8},{8,12},{1,5},{5,9},{9,13},{2,6},{6,10},{10,14},{3,7},{... | collective-permute-start | bytes 552968 | tf_op jit(solution)/shard_map/while/body/eval_jaxpr/ppermute | solution.py:16
  151.2 6.8 %collective-permute-start = (bf16[64,512]{0,1:T(8,128)(2,1)}, bf16[64,512]{0,1:T(8,128)(2,1)S(1)}, u32[]{:S(2)}, u32[]{:S(2)}) collective-permute-start(bf16[64,512]{0,1:T(8,128)(2,1)} %get-tuple-element.718), channel_id=1, source_target_pairs={{0,2},{1,3},{4,6},{5,7},{8,10},{9,11},{12,14},{13,15},{16,18},{17,... | collective-permute-start | bytes 196616 | tf_op jit(solution)/shard_map/while/body/eval_jaxpr/ppermute | solution.py:16
  154.2 3.8 %collective-permute-start.1 = (bf16[64,512]{0,1:T(8,128)(2,1)}, bf16[64,512]{0,1:T(8,128)(2,1)S(1)}, u32[]{:S(2)}, u32[]{:S(2)}) collective-permute-start(bf16[64,512]{0,1:T(8,128)(2,1)} %get-tuple-element.718), channel_id=1, source_target_pairs={{0,1},{1,2},{2,3},{4,5},{5,6},{6,7},{8,9},{9,10},{10,11},{12,13},{... | collective-permute-start | bytes 196616 | tf_op jit(solution)/shard_map/while/body/eval_jaxpr/ppermute | solution.py:16
  158.0 52.5 %collective-permute-start.2 = (bf16[64,1440]{1,0:T(8,128)(2,1)S(1)}, bf16[64,1440]{1,0:T(8,128)(2,1)S(1)}, u32[]{:S(2)}, u32[]{:S(2)}) collective-permute-start(bf16[64,1440]{1,0:T(8,128)(2,1)S(1)} %get-tuple-element.793), channel_id=1, source_target_pairs={{0,4},{4,8},{8,12},{1,5},{5,9},{9,13},{2,6},{6,10},{10,14},{3,7},{... | collective-permute-start | bytes 552968 | tf_op jit(solution)/shard_map/while/body/eval_jaxpr/ppermute | solution.py:16
  223.2 6.9 %collective-permute-start = (bf16[64,512]{0,1:T(8,128)(2,1)}, bf16[64,512]{0,1:T(8,128)(2,1)S(1)}, u32[]{:S(2)}, u32[]{:S(2)}) collective-permute-start(bf16[64,512]{0,1:T(8,128)(2,1)} %get-tuple-element.718), channel_id=1, source_target_pairs={{0,2},{1,3},{4,6},{5,7},{8,10},{9,11},{12,14},{13,15},{16,18},{17,... | collective-permute-start | bytes 196616 | tf_op jit(solution)/shard_map/while/body/eval_jaxpr/ppermute | solution.py:16
  225.5 4.6 %collective-permute-start.1 = (bf16[64,512]{0,1:T(8,128)(2,1)}, bf16[64,512]{0,1:T(8,128)(2,1)S(1)}, u32[]{:S(2)}, u32[]{:S(2)}) collective-permute-start(bf16[64,512]{0,1:T(8,128)(2,1)} %get-tuple-element.718), channel_id=1, source_target_pairs={{0,1},{1,2},{2,3},{4,5},{5,6},{6,7},{8,9},{9,10},{10,11},{12,13},{... | collective-permute-start | bytes 196616 | tf_op jit(solution)/shard_map/while/body/eval_jaxpr/ppermute | solution.py:16
  233.8 2.2 slice-start
  234.7 2.2 slice-start.1
  238.2 9.1 %collective-permute-start.2 = (bf16[64,1440]{1,0:T(8,128)(2,1)S(1)}, bf16[64,1440]{1,0:T(8,128)(2,1)S(1)}, u32[]{:S(2)}, u32[]{:S(2)}) collective-permute-start(bf16[64,1440]{1,0:T(8,128)(2,1)S(1)} %get-tuple-element.793), channel_id=1, source_target_pairs={{0,4},{4,8},{8,12},{1,5},{5,9},{9,13},{2,6},{6,10},{10,14},{3,7},{... | collective-permute-start | bytes 552968 | tf_op jit(solution)/shard_map/while/body/eval_jaxpr/ppermute | solution.py:16
  260.0 6.9 %collective-permute-start = (bf16[64,512]{0,1:T(8,128)(2,1)}, bf16[64,512]{0,1:T(8,128)(2,1)S(1)}, u32[]{:S(2)}, u32[]{:S(2)}) collective-permute-start(bf16[64,512]{0,1:T(8,128)(2,1)} %get-tuple-element.718), channel_id=1, source_target_pairs={{0,2},{1,3},{4,6},{5,7},{8,10},{9,11},{12,14},{13,15},{16,18},{17,... | collective-permute-start | bytes 196616 | tf_op jit(solution)/shard_map/while/body/eval_jaxpr/ppermute | solution.py:16
  262.3 4.6 %collective-permute-start.1 = (bf16[64,512]{0,1:T(8,128)(2,1)}, bf16[64,512]{0,1:T(8,128)(2,1)S(1)}, u32[]{:S(2)}, u32[]{:S(2)}) collective-permute-start(bf16[64,512]{0,1:T(8,128)(2,1)} %get-tuple-element.718), channel_id=1, source_target_pairs={{0,1},{1,2},{2,3},{4,5},{5,6},{6,7},{8,9},{9,10},{10,11},{12,13},{... | collective-permute-start | bytes 196616 | tf_op jit(solution)/shard_map/while/body/eval_jaxpr/ppermute | solution.py:16
  270.6 2.2 slice-start
  271.5 2.2 slice-start.1
  274.9 9.1 %collective-permute-start.2 = (bf16[64,1440]{1,0:T(8,128)(2,1)S(1)}, bf16[64,1440]{1,0:T(8,128)(2,1)S(1)}, u32[]{:S(2)}, u32[]{:S(2)}) collective-permute-start(bf16[64,1440]{1,0:T(8,128)(2,1)S(1)} %get-tuple-element.793), channel_id=1, source_target_pairs={{0,4},{4,8},{8,12},{1,5},{5,9},{9,13},{2,6},{6,10},{10,14},{3,7},{... | collective-permute-start | bytes 552968 | tf_op jit(solution)/shard_map/while/body/eval_jaxpr/ppermute | solution.py:16
  296.7 6.9 %collective-permute-start = (bf16[64,512]{0,1:T(8,128)(2,1)}, bf16[64,512]{0,1:T(8,128)(2,1)S(1)}, u32[]{:S(2)}, u32[]{:S(2)}) collective-permute-start(bf16[64,512]{0,1:T(8,128)(2,1)} %get-tuple-element.718), channel_id=1, source_target_pairs={{0,2},{1,3},{4,6},{5,7},{8,10},{9,11},{12,14},{13,15},{16,18},{17,... | collective-permute-start | bytes 196616 | tf_op jit(solution)/shard_map/while/body/eval_jaxpr/ppermute | solution.py:16
  299.0 4.6 %collective-permute-start.1 = (bf16[64,512]{0,1:T(8,128)(2,1)}, bf16[64,512]{0,1:T(8,128)(2,1)S(1)}, u32[]{:S(2)}, u32[]{:S(2)}) collective-permute-start(bf16[64,512]{0,1:T(8,128)(2,1)} %get-tuple-element.718), channel_id=1, source_target_pairs={{0,1},{1,2},{2,3},{4,5},{5,6},{6,7},{8,9},{9,10},{10,11},{12,13},{... | collective-permute-start | bytes 196616 | tf_op jit(solution)/shard_map/while/body/eval_jaxpr/ppermute | solution.py:16
  307.3 2.2 slice-start
  308.2 2.2 slice-start.1
  311.7 9.1 %collective-permute-start.2 = (bf16[64,1440]{1,0:T(8,128)(2,1)S(1)}, bf16[64,1440]{1,0:T(8,128)(2,1)S(1)}, u32[]{:S(2)}, u32[]{:S(2)}) collective-permute-start(bf16[64,1440]{1,0:T(8,128)(2,1)S(1)} %get-tuple-element.793), channel_id=1, source_target_pairs={{0,4},{4,8},{8,12},{1,5},{5,9},{9,13},{2,6},{6,10},{10,14},{3,7},{... | collective-permute-start | bytes 552968 | tf_op jit(solution)/shard_map/while/body/eval_jaxpr/ppermute | solution.py:16
  333.5 6.9 %collective-permute-start = (bf16[64,512]{0,1:T(8,128)(2,1)}, bf16[64,512]{0,1:T(8,128)(2,1)S(1)}, u32[]{:S(2)}, u32[]{:S(2)}) collective-permute-start(bf16[64,512]{0,1:T(8,128)(2,1)} %get-tuple-element.718), channel_id=1, source_target_pairs={{0,2},{1,3},{4,6},{5,7},{8,10},{9,11},{12,14},{13,15},{16,18},{17,... | collective-permute-start | bytes 196616 | tf_op jit(solution)/shard_map/while/body/eval_jaxpr/ppermute | solution.py:16
  335.8 4.6 %collective-permute-start.1 = (bf16[64,512]{0,1:T(8,128)(2,1)}, bf16[64,512]{0,1:T(8,128)(2,1)S(1)}, u32[]{:S(2)}, u32[]{:S(2)}) collective-permute-start(bf16[64,512]{0,1:T(8,128)(2,1)} %get-tuple-element.718), channel_id=1, source_target_pairs={{0,1},{1,2},{2,3},{4,5},{5,6},{6,7},{8,9},{9,10},{10,11},{12,13},{... | collective-permute-start | bytes 196616 | tf_op jit(solution)/shard_map/while/body/eval_jaxpr/ppermute | solution.py:16
  344.1 2.2 slice-start
  345.0 2.2 slice-start.1
  348.4 8.8 %collective-permute-start.2 = (bf16[64,1440]{1,0:T(8,128)(2,1)S(1)}, bf16[64,1440]{1,0:T(8,128)(2,1)S(1)}, u32[]{:S(2)}, u32[]{:S(2)}) collective-permute-start(bf16[64,1440]{1,0:T(8,128)(2,1)S(1)} %get-tuple-element.793), channel_id=1, source_target_pairs={{0,4},{4,8},{8,12},{1,5},{5,9},{9,13},{2,6},{6,10},{10,14},{3,7},{... | collective-permute-start | bytes 552968 | tf_op jit(solution)/shard_map/while/body/eval_jaxpr/ppermute | solution.py:16
Sparse Core Ops, SparseCore 0:
  9.5 45.0 all-gather.5
  56.2 46.3 all-gather.3
